TPU v7x, 32 devices: a whole 2x2x4 slice. The times are simulated.
32 devices in a mesh: row: 4 (over x, core), col: 8 (over z, y).
Axes of the slice: x: 2, y: 2, z: 4, core: 2. Of those that a mesh axis runs over, the one named last changes fastest.
Arguments:
- points: float32 [16, 8192], P(None, ('row', 'col')), may hold values from -6 to 6
- lengthscale: float32 [16], replicated, may hold values from 2 to 8
- signal: float32 [1], replicated, may hold values from 0.5 to 2
- noise: float32 [1], replicated, may hold values from 0.05 to 0.5
- targets: float32 [8192], P(('row', 'col')), may hold values from -12 to 12
- probe_bits: int32 [31, 8192], P(None, ('row', 'col')), may hold values from 0 to 1
Outputs:
- solution: float32 [32, 8192], P(None, ('row', 'col'))
- residual: float32 [32, 8192], P(None, ('row', 'col'))
All inputs are finite; a program needn't handle non-finite values.
Results may differ from a plain program's by a relative error of at most 0.0013.
Values sent between devices are 32-bit elements; how exact they have to be, the bound alone decides.
No kernel may reach another device: no remote copies, remote signals or barrier semaphores. Data moves between devices by JAX's collectives and lax.ppermute only.
A program may use at most 128 MiB of HBM per device.

v0:
```python
import jax
import jax.numpy as jnp
from jax import lax
from jax.sharding import PartitionSpec as P

ITERS = 3
ROOT_FIVE = 5.0**0.5


def matern_tile(row_scaled, col_scaled, signal_value):
    row_sq = jnp.sum(row_scaled * row_scaled, axis=0)
    col_sq = jnp.sum(col_scaled * col_scaled, axis=0)
    cross_term = lax.dot_general(
        row_scaled,
        col_scaled,
        (((0,), (0,)), ((), ())),
        precision=lax.Precision.HIGHEST,
        preferred_element_type=jnp.float32,
    )
    dist_sq = jnp.maximum(row_sq[:, None] + col_sq[None, :] - 2.0 * cross_term, 0.0)
    radius = jnp.sqrt(dist_sq)
    return (
        signal_value
        * (1.0 + ROOT_FIVE * radius + 5.0 / 3.0 * dist_sq)
        * jnp.exp(-ROOT_FIVE * radius)
    )


def row_blocks(row_scaled):
    row_total = row_scaled.shape[1]
    block_rows = min(1024, row_total)
    block_count = row_total // block_rows
    return row_scaled.reshape(row_scaled.shape[0], block_count, block_rows).transpose(1, 0, 2)


def apply_tile(row_scaled, col_scaled, signal_value, vectors):
    row_total = row_scaled.shape[1]
    stacked = row_blocks(row_scaled)

    def one_block(row_block):
        kernel_tile = matern_tile(row_block, col_scaled, signal_value)
        return lax.dot_general(
            vectors,
            kernel_tile,
            (((1,), (1,)), ((), ())),
            precision=lax.Precision.HIGHEST,
            preferred_element_type=jnp.float32,
        )

    pieces = lax.map(one_block, stacked)
    return pieces.transpose(1, 0, 2).reshape(vectors.shape[0], row_total)


def squares(residual):
    return lax.psum(jnp.sum(residual * residual, axis=1), ("row", "col"))


def body(points, lengthscale, signal, noise, targets, probe_bits):
    scaled = points / lengthscale[:, None]
    signs = 2.0 * probe_bits.astype(jnp.float32) - 1.0
    right_side = jnp.concatenate([targets[None, :], signs], axis=0)
    signal_value = signal[0]
    noise_value = noise[0]
    every_point = lax.all_gather(scaled, ("row", "col"), axis=1, tiled=True)
    solution = jnp.zeros_like(right_side)
    residual = right_side
    direction = right_side
    norm_now = squares(residual)
    for step in range(ITERS):
        summed = apply_tile(
            scaled,
            every_point,
            signal_value,
            lax.all_gather(direction, ("row", "col"), axis=1, tiled=True),
        )
        image = summed + noise_value * direction
        curved = lax.psum(jnp.sum(direction * image, axis=1), ("row", "col"))
        alpha = norm_now / curved
        solution = solution + alpha[:, None] * direction
        residual = residual - alpha[:, None] * image
        if step + 1 < ITERS:
            norm_next = squares(residual)
            direction = residual + (norm_next / norm_now)[:, None] * direction
            norm_now = norm_next
    return (solution, residual)


def solution(mesh):
    return jax.shard_map(
        body,
        mesh=mesh,
        in_specs=(
            P(None, ("row", "col")),
            P(),
            P(),
            P(),
            P(("row", "col")),
            P(None, ("row", "col")),
        ),
        out_specs=(P(None, ("row", "col")), P(None, ("row", "col"))),
        check_vma=False,
    )
```

profile of v0, /device:TPU:0, one launch (start us, length us, event | category | flops | bytes accessed | tf_op | source)
XLA Modules:
  0.0 442.8 jit_solution(3945853298160864915)
XLA Ops:
  7.2 0.0 all-gather.4.cloned.1.call-start
  7.2 0.8 multiply_add_fusion.3
  8.0 1.3 pad_maximum_fusion
  9.3 0.0 all-gather.6.cloned.1.call-start
  10.6 0.8 multiply_reduce_fusion.7
  11.5 73.2 %all_gather.13 = f32[16,8192]{1,0:T(8,128)S(1)} all-gather(f32[16,256]{1,0:T(8,128)S(1)} %get-tuple-element.51), channel_id=1, replica_groups=mesh['row'=4,'col'=8] {'row','col'}, dimensions={1}, use_global_device_ids=true | all-gather | bytes 540672 | tf_op jit(solution)/shard_map/all_gather | solution.py:64
  84.6 0.1 multiply_reduce_fusion
  84.7 14.0 %exponential_multiply_fusion = f32[256,8192]{1,0:T(8,128)} fusion(f32[16,256]{1,0:T(8,128)S(1)} %get-tuple-element.51, f32[16,8192]{1,0:T(8,128)S(1)} %all_gather.13, f32[8192]{0:T(1024)S(1)} %multiply_reduce_fusion, f32[256]{0:T(256)S(1)} %get-tuple-element.50, f32[]{:T(128)} %bitcast.11), kind=kOutput, calls=%fused_computation.3 | convolution fusion | flops 425721856 | bytes 8963076 | tf_op jit(solution)/shard_map/while/body/eval_jaxpr/dot_general | solution.py:13
  98.8 11.2 %multiply_reduce_fusion.5 = (f32[32]{0:T(128)S(1)}, f32[32]{0:T(128)S(1)}, f32[32,256]{1,0:T(8,128)S(1)}) fusion(f32[32,256]{1,0:T(8,128)S(1)} %copy-done.2, f32[]{:T(128)} %bitcast.12, f32[32,8192]{1,0:T(8,128)} %all-gather.4.cloned.1.call-done, f32[256,8192]{1,0:T(8,128)} %exponential_multiply_fusion), kind=kOutput, calls=%fused_computation.19 | convolution fusion | flops 805355456 | bytes 9502980 | tf_op jit(solution)/shard_map/while/body/eval_jaxpr/dot_general | solution.py:42
  109.9 37.1 %all-reduce = (f32[32]{0:T(128)S(1)}, f32[32]{0:T(128)S(1)}) all-reduce(f32[32]{0:T(128)S(1)} %get-tuple-element.39, f32[32]{0:T(128)S(1)} %get-tuple-element.38), channel_id=1, replica_groups=mesh['row'=4,'col'=8] {'row','col'}, use_global_device_ids=true, to_apply=%region_1.0 | all-reduce | flops 64 | bytes 512 | tf_op jit(solution)/shard_map/psum | solution.py:55
  147.0 0.2 multiply_reduce_fusion.4
  147.2 41.5 %psum.44 = f32[32]{0:T(128)S(1)} all-reduce(f32[32]{0:T(128)S(1)} %multiply_reduce_fusion.4), channel_id=1, replica_groups=mesh['row'=4,'col'=8] {'row','col'}, use_global_device_ids=true, to_apply=%region_7.8 | all-reduce | flops 32 | bytes 256 | tf_op jit(solution)/shard_map/psum | solution.py:55
  188.7 0.7 multiply_add_fusion.2
  189.5 0.0 all-gather.8.cloned.1.call-start
  189.5 51.3 %all-gather.6.cloned.1.call-done = f32[32,8192]{1,0:T(8,128)} async-done(((f32[32,256]{1,0:T(8,128)}), f32[32,8192]{1,0:T(8,128)}) %all-gather.6.cloned.1.call-update) | async-done | bytes 1048592 | tf_op jit(solution)/shard_map/all_gather | solution.py:74
  240.8 11.1 %multiply_reduce_fusion.3 = (f32[32]{0:T(128)S(1)}, f32[32,256]{1,0:T(8,128)S(1)}) fusion(f32[32,256]{1,0:T(8,128)} %multiply_add_fusion.2, f32[]{:T(128)} %bitcast.14, f32[32,8192]{1,0:T(8,128)} %all-gather.6.cloned.1.call-done, f32[256,8192]{1,0:T(8,128)} %exponential_multiply_fusion), kind=kOutput, calls=%fused_computation.15 | convolution fusion | flops 805339136 | bytes 9502852 | tf_op jit(solution)/shard_map/while/body/eval_jaxpr/dot_general | solution.py:42
  251.9 40.3 %psum.45 = f32[32]{0:T(128)S(1)} all-reduce(f32[32]{0:T(128)S(1)} %get-tuple-element.61), channel_id=1, replica_groups=mesh['row'=4,'col'=8] {'row','col'}, use_global_device_ids=true, to_apply=%region_9.10 | all-reduce | flops 32 | bytes 256 | tf_op jit(solution)/shard_map/psum | solution.py:77
  292.1 0.2 multiply_reduce_fusion.2
  292.3 39.2 %psum.46 = f32[32]{0:T(128)S(1)} all-reduce(f32[32]{0:T(128)S(1)} %get-tuple-element.48), channel_id=1, replica_groups=mesh['row'=4,'col'=8] {'row','col'}, use_global_device_ids=true, to_apply=%region_11.12 | all-reduce | flops 32 | bytes 256 | tf_op jit(solution)/shard_map/psum | solution.py:55
  331.5 0.7 multiply_add_fusion.1
  332.3 52.0 %all-gather.8.cloned.1.call-done = f32[32,8192]{1,0:T(8,128)} async-done(((f32[32,256]{1,0:T(8,128)}), f32[32,8192]{1,0:T(8,128)}) %all-gather.8.cloned.1.call-update) | async-done | bytes 1048592 | tf_op jit(solution)/shard_map/all_gather | solution.py:74
  384.2 11.1 %multiply_reduce_fusion.1 = (f32[32]{0:T(128)S(1)}, f32[32,256]{1,0:T(8,128)S(1)}) fusion(f32[32,256]{1,0:T(8,128)} %multiply_add_fusion.1, f32[]{:T(128)} %bitcast.13, f32[32,8192]{1,0:T(8,128)} %all-gather.8.cloned.1.call-done, f32[256,8192]{1,0:T(8,128)} %exponential_multiply_fusion), kind=kOutput, calls=%fused_computation.11 | convolution fusion | flops 805339136 | bytes 9502852 | tf_op jit(solution)/shard_map/while/body/eval_jaxpr/dot_general | solution.py:42
  395.3 40.3 %psum.47 = f32[32]{0:T(128)S(1)} all-reduce(f32[32]{0:T(128)S(1)} %get-tuple-element.63), channel_id=1, replica_groups=mesh['row'=4,'col'=8] {'row','col'}, use_global_device_ids=true, to_apply=%region_13.14 | all-reduce | flops 32 | bytes 256 | tf_op jit(solution)/shard_map/psum | solution.py:77
  435.5 0.7 multiply_subtract_fusion
  (17 shorter events, 0.1 us)
Async XLA Ops:
  7.2 91.6 %all-gather.4.cloned.1.call-start = ((), (), s32[]{:S(2)}) async-start(), calls=%async_computation | async-start | bytes 1081344 | tf_op jit(solution)/shard_map/all_gather | solution.py:74
  9.3 231.5 %all-gather.6.cloned.1.call-start = ((), (), s32[]{:S(2)}) async-start(), calls=%async_computation.1 | async-start | bytes 1081344 | tf_op jit(solution)/shard_map/all_gather | solution.py:74
  84.7 14.0 %copy-start.2 = (f32[32,256]{1,0:T(8,128)S(1)}, f32[32,256]{1,0:T(8,128)}, u32[]{:S(2)}) copy-start(f32[32,256]{1,0:T(8,128)} %pad_maximum_fusion) | copy-start | bytes 98308
  98.7 48.3 %copy-start.3 = (f32[256]{0:T(256)S(1)}, f32[256]{0:T(256)}, u32[]{:S(2)}) copy-start(f32[256]{0:T(256)} %param.10) | copy-start | bytes 3076
  189.4 142.1 %copy-start = (f32[32,256]{1,0:T(8,128)S(1)}, f32[32,256]{1,0:T(8,128)}, u32[]{:S(2)}) copy-start(f32[32,256]{1,0:T(8,128)} %multiply_add_fusion.2) | copy-start | bytes 98308
  189.5 194.7 %all-gather.8.cloned.1.call-start = ((), (), s32[]{:S(2)}) async-start(), calls=%async_computation.2 | async-start | bytes 1081344 | tf_op jit(solution)/shard_map/all_gather | solution.py:74
  332.2 103.3 %copy-start.1 = (f32[32,256]{1,0:T(8,128)S(1)}, f32[32,256]{1,0:T(8,128)}, u32[]{:S(2)}) copy-start(f32[32,256]{1,0:T(8,128)} %multiply_add_fusion.1) | copy-start | bytes 98308
Sparse Core Ops, SparseCore 0:
  11.4 54.6 all-gather.3
  189.6 51.1 all-gather.5
  332.4 51.7 all-gather.7
where the time goes:
time: 444 us; the launch traced here: 443 us
  blocking collectives  272 us (61%)
  waiting for transfers between devices  103 us (23%)
  matrix products  47.3 us (11%)
  between operations  15.1 us (3%)
  other arithmetic  5.46 us (1%)
    psum x3, blocking collectives, squares(): return lax.psum(jnp.sum(residual * residual, axis=1), ('row', 'col'))  118 us
    all_gather x3, waiting for transfers between devices, body(): lax.all_gather(direction, ('row', 'col'), axis=1, tiled=True)  103 us
    psum x2, blocking collectives, body(): curved = lax.psum(jnp.sum(direction * image, axis=1), ('row', 'col'))  80.5 us
    all_gather x1, blocking collectives, body(): every_point = lax.all_gather(scaled, ('row', 'col'), axis=1, tiled=True)  73.2 us
    dot_general x3, matrix products, one_block(): lax.dot_general(vectors, kernel_tile, (((1,), (1,)), ((), ())), precision...  33.3 us
    dot_general x1, matrix products, matern_tile(): lax.dot_general(row_scaled, col_scaled, (((0,), (0,)), ((), ())), precisi...  14 us
  transfers between devices with their start and end apart: 3, of which 2 were waited for; matrix products, arithmetic and copies ran while one was open for 3% of the time, Pallas kernels for 0%

commit v1 on v0

--- a/solution.py
+++ b/solution.py
@@ -74,7 +74,7 @@
             lax.all_gather(direction, ("row", "col"), axis=1, tiled=True),
         )
         image = summed + noise_value * direction
-        curved = lax.psum(jnp.sum(direction * image, axis=1), ("row", "col"))
+        curved = jnp.sum(lax.all_gather(jnp.sum(direction * image, axis=1), ("row", "col")), axis=0)
         alpha = norm_now / curved
         solution = solution + alpha[:, None] * direction
         residual = residual - alpha[:, None] * image

time: 444 us -> 445 us (level)
    unnamed x0 -> x2, blocking collectives: none -> 80.5 us
    psum x2 -> x0, blocking collectives: 80.5 us -> none  [body(): curved = lax.psum(jnp.sum(direction * image, axis=1), ('row', 'col'))]
where the time goes in v1:
time: 445 us; the launch traced here: 444 us
  blocking collectives  271 us (61%)
  waiting for transfers between devices  103 us (23%)
  matrix products  47.3 us (11%)
  between operations  15.1 us (3%)
  other arithmetic  5.54 us (1%)
    psum x3, blocking collectives, squares(): return lax.psum(jnp.sum(residual * residual, axis=1), ('row', 'col'))  118 us
    all_gather x3, waiting for transfers between devices, body(): lax.all_gather(direction, ('row', 'col'), axis=1, tiled=True)  103 us
    unnamed x2, blocking collectives  80.5 us
    all_gather x1, blocking collectives, body(): every_point = lax.all_gather(scaled, ('row', 'col'), axis=1, tiled=True)  73.2 us
    dot_general x3, matrix products, one_block(): lax.dot_general(vectors, kernel_tile, (((1,), (1,)), ((), ())), precision...  33.3 us
    dot_general x1, matrix products, matern_tile(): lax.dot_general(row_scaled, col_scaled, (((0,), (0,)), ((), ())), precisi...  14 us
  transfers between devices with their start and end apart: 3, of which 2 were waited for; matrix products, arithmetic and copies ran while one was open for 3% of the time, Pallas kernels for 0%

profile of v1, /device:TPU:0, one launch (start us, length us, event | category | flops | bytes accessed | tf_op | source)
XLA Modules:
  0.0 443.8 jit_solution(6436264020442863955)
XLA Ops:
  7.2 0.8 multiply_add_fusion.3
  8.0 1.3 pad_maximum_fusion
  10.6 0.8 multiply_reduce_fusion.7
  11.5 73.2 %all_gather.31 = f32[16,8192]{1,0:T(8,128)S(1)} all-gather(f32[16,256]{1,0:T(8,128)S(1)} %get-tuple-element.51), channel_id=1, replica_groups=mesh['row'=4,'col'=8] {'row','col'}, dimensions={1}, use_global_device_ids=true | all-gather | bytes 540672 | tf_op jit(solution)/shard_map/all_gather | solution.py:64
  84.6 0.1 multiply_reduce_fusion
  84.7 14.0 %exponential_multiply_fusion = f32[256,8192]{1,0:T(8,128)} fusion(f32[16,256]{1,0:T(8,128)S(1)} %get-tuple-element.51, f32[16,8192]{1,0:T(8,128)S(1)} %all_gather.31, f32[8192]{0:T(1024)S(1)} %multiply_reduce_fusion, f32[256]{0:T(256)S(1)} %get-tuple-element.50, f32[]{:T(128)} %bitcast.11), kind=kOutput, calls=%fused_computation.3 | convolution fusion | flops 425721856 | bytes 8963076 | tf_op jit(solution)/shard_map/while/body/eval_jaxpr/dot_general | solution.py:13
  98.7 11.2 %multiply_reduce_fusion.5 = (f32[32]{0:T(128)S(1)}, f32[32]{0:T(128)S(1)}, f32[32,256]{1,0:T(8,128)S(1)}) fusion(f32[32,256]{1,0:T(8,128)S(1)} %copy-done.2, f32[]{:T(128)} %bitcast.12, f32[32,8192]{1,0:T(8,128)} %all-gather.7.cloned.1.call-done, f32[256,8192]{1,0:T(8,128)} %exponential_multiply_fusion), kind=kOutput, calls=%fused_computation.19 | convolution fusion | flops 805355456 | bytes 9502980 | tf_op jit(solution)/shard_map/while/body/eval_jaxpr/dot_general | solution.py:42
  109.9 0.2 dynamic-update-slice
  110.2 37.1 %all-reduce.3 = (f32[32]{0:T(128)S(1)}, f32[1024]{0:T(1024)S(1)}) all-reduce(f32[32]{0:T(128)S(1)} %get-tuple-element.39, f32[1024]{0:T(1024)S(1)} %dynamic-update-slice), channel_id=1, replica_groups=mesh['row'=4,'col'=8] {'row','col'}, use_global_device_ids=true, to_apply=%region_1.0 | all-reduce | flops 1056 | bytes 8448 | tf_op jit(solution)/shard_map/psum | solution.py:55
  147.4 0.2 multiply_reduce_fusion.4
  147.6 41.5 %psum.22 = f32[32]{0:T(128)S(1)} all-reduce(f32[32]{0:T(128)S(1)} %multiply_reduce_fusion.4), channel_id=1, replica_groups=mesh['row'=4,'col'=8] {'row','col'}, use_global_device_ids=true, to_apply=%region_7.8 | all-reduce | flops 32 | bytes 256 | tf_op jit(solution)/shard_map/psum | solution.py:55
  189.1 0.7 multiply_add_fusion.2
  189.9 51.3 %all-gather.9.cloned.1.call-done = f32[32,8192]{1,0:T(8,128)} async-done(((f32[32,256]{1,0:T(8,128)}), f32[32,8192]{1,0:T(8,128)}) %all-gather.9.cloned.1.call-update) | async-done | bytes 1048592 | tf_op jit(solution)/shard_map/all_gather | solution.py:74
  241.2 11.1 %multiply_reduce_fusion.3 = (f32[32]{0:T(128)S(1)}, f32[32,256]{1,0:T(8,128)S(1)}) fusion(f32[32,256]{1,0:T(8,128)} %multiply_add_fusion.2, f32[]{:T(128)} %bitcast.14, f32[32,8192]{1,0:T(8,128)} %all-gather.9.cloned.1.call-done, f32[256,8192]{1,0:T(8,128)} %exponential_multiply_fusion), kind=kOutput, calls=%fused_computation.15 | convolution fusion | flops 805339136 | bytes 9502852 | tf_op jit(solution)/shard_map/while/body/eval_jaxpr/dot_general | solution.py:42
  252.3 0.2 dynamic-update-slice.1
  252.5 40.3 %all-reduce.1 = f32[1024]{0:T(1024)S(1)} all-reduce(f32[1024]{0:T(1024)S(1)} %dynamic-update-slice.1), channel_id=3, replica_groups=mesh['row'=4,'col'=8] {'row','col'}, use_global_device_ids=true, to_apply=%add.1 | all-reduce | flops 1024 | bytes 8192
  292.9 0.2 multiply_reduce_fusion.2
  293.1 39.2 %psum.23 = f32[32]{0:T(128)S(1)} all-reduce(f32[32]{0:T(128)S(1)} %get-tuple-element.48), channel_id=1, replica_groups=mesh['row'=4,'col'=8] {'row','col'}, use_global_device_ids=true, to_apply=%region_11.12 | all-reduce | flops 32 | bytes 256 | tf_op jit(solution)/shard_map/psum | solution.py:55
  332.3 0.7 multiply_add_fusion.1
  333.0 52.0 %all-gather.11.cloned.1.call-done = f32[32,8192]{1,0:T(8,128)} async-done(((f32[32,256]{1,0:T(8,128)}), f32[32,8192]{1,0:T(8,128)}) %all-gather.11.cloned.1.call-update) | async-done | bytes 1048592 | tf_op jit(solution)/shard_map/all_gather | solution.py:74
  384.9 11.1 %multiply_reduce_fusion.1 = (f32[32]{0:T(128)S(1)}, f32[32,256]{1,0:T(8,128)S(1)}) fusion(f32[32,256]{1,0:T(8,128)} %multiply_add_fusion.1, f32[]{:T(128)} %bitcast.13, f32[32,8192]{1,0:T(8,128)} %all-gather.11.cloned.1.call-done, f32[256,8192]{1,0:T(8,128)} %exponential_multiply_fusion), kind=kOutput, calls=%fused_computation.11 | convolution fusion | flops 805339136 | bytes 9502852 | tf_op jit(solution)/shard_map/while/body/eval_jaxpr/dot_general | solution.py:42
  396.0 0.2 dynamic-update-slice.2
  396.3 40.2 %all-reduce.2 = f32[1024]{0:T(1024)S(1)} all-reduce(f32[1024]{0:T(1024)S(1)} %dynamic-update-slice.2), channel_id=4, replica_groups=mesh['row'=4,'col'=8] {'row','col'}, use_global_device_ids=true, to_apply=%add.2 | all-reduce | flops 1024 | bytes 8192
  436.6 0.7 multiply_subtract_fusion
  (29 shorter events, 0.5 us)
Async XLA Ops:
  7.2 91.6 %all-gather.7.cloned.1.call-start = ((), (), s32[]{:S(2)}) async-start(), calls=%async_computation | async-start | bytes 1081344 | tf_op jit(solution)/shard_map/all_gather | solution.py:74
  9.3 231.9 %all-gather.9.cloned.1.call-start = ((), (), s32[]{:S(2)}) async-start(), calls=%async_computation.1 | async-start | bytes 1081344 | tf_op jit(solution)/shard_map/all_gather | solution.py:74
  84.7 14.0 %copy-start.2 = (f32[32,256]{1,0:T(8,128)S(1)}, f32[32,256]{1,0:T(8,128)}, u32[]{:S(2)}) copy-start(f32[32,256]{1,0:T(8,128)} %pad_maximum_fusion) | copy-start | bytes 98308
  98.7 48.7 %copy-start.3 = (f32[256]{0:T(256)S(1)}, f32[256]{0:T(256)}, u32[]{:S(2)}) copy-start(f32[256]{0:T(256)} %param.10) | copy-start | bytes 3076
  189.8 142.4 %copy-start = (f32[32,256]{1,0:T(8,128)S(1)}, f32[32,256]{1,0:T(8,128)}, u32[]{:S(2)}) copy-start(f32[32,256]{1,0:T(8,128)} %multiply_add_fusion.2) | copy-start | bytes 98308
  189.8 195.1 %all-gather.11.cloned.1.call-start = ((), (), s32[]{:S(2)}) async-start(), calls=%async_computation.2 | async-start | bytes 1081344 | tf_op jit(solution)/shard_map/all_gather | solution.py:74
  333.0 103.6 %copy-start.1 = (f32[32,256]{1,0:T(8,128)S(1)}, f32[32,256]{1,0:T(8,128)}, u32[]{:S(2)}) copy-start(f32[32,256]{1,0:T(8,128)} %multiply_add_fusion.1) | copy-start | bytes 98308
Sparse Core Ops, SparseCore 0:
  11.4 54.6 all-gather.6
  190.0 51.1 all-gather.8
  333.1 51.7 all-gather.10
